TPU v7x, 32 devices: a 4x4x1 block of a 4x4x8 slice. The times are simulated.
32 devices in a mesh: dp: 1 (over z), sp: 32 (over y, x, core).
Axes of the slice: x: 4, y: 4, z: 1, core: 2. Of those that a mesh axis runs over, the one named last changes fastest.
The devices are a block of a 4x4x8 slice.
Arguments:
- x: bfloat16 [4, 8192], P('dp')
- wq: bfloat16 [8192, 8192], replicated
- wk: bfloat16 [8192, 1024], replicated
- wv: bfloat16 [8192, 1024], replicated
- wo: bfloat16 [8192, 8192], P('sp')
- kc: bfloat16 [4, 32768, 8, 128], P('dp', 'sp')
- vc: bfloat16 [4, 32768, 8, 128], P('dp', 'sp')
- pos: int32 [4], P('dp')
- lens: int32 [4], P('dp')
Outputs:
- output 1: bfloat16 [4, 8192], P('dp')
- output 2: bfloat16 [4, 32768, 8, 128], P('dp', 'sp')
- output 3: bfloat16 [4, 32768, 8, 128], P('dp', 'sp')
All inputs are finite; a program needn't handle non-finite values.
Results may differ from a plain program's by a relative error of at most 0.00358209.
Values are sent between devices in bfloat16 or wider.
A program may use at most 768 MiB of HBM per device.

v0:
```python
import jax
import jax.numpy as jnp
from jax import lax
from jax.sharding import PartitionSpec as P


def solution(mesh):
    f32 = jnp.float32
    bf16 = jnp.bfloat16

    def local(x, wq, wk, wv, wo, kc, vc, pos, lens):
        n = x.shape[0]
        _, sl, hkvv, dh = kc.shape
        h = wq.shape[1] // dh
        g = h // hkvv
        me = lax.axis_index('sp')
        q = jnp.dot(x, wq, preferred_element_type=f32).astype(bf16).reshape(n, hkvv, g, 1, dh)
        k = jnp.dot(x, wk, preferred_element_type=f32).astype(bf16).reshape(n, 1, hkvv, dh)
        v = jnp.dot(x, wv, preferred_element_type=f32).astype(bf16).reshape(n, 1, hkvv, dh)
        start = me * sl
        tpos = start + jnp.arange(sl)
        hit = (tpos[None, :] == pos[:, None])[:, :, None, None]
        kc = jnp.where(hit, k, kc)
        vc = jnp.where(hit, v, vc)
        eye = jnp.eye(hkvv, dtype=bool)[:, None, :, None]
        qb = jnp.where(eye, q, jnp.zeros((), bf16)).reshape(n, h, hkvv, dh)
        s = jnp.einsum('bjkd,bskd->bjs', qb, kc, preferred_element_type=f32) * dh ** -0.5
        valid = tpos[None, :] < lens[:, None]
        s = jnp.where(valid[:, None, :], s, -jnp.inf)
        m = s.max(-1)
        p = jnp.exp(s - jnp.where(jnp.isfinite(m), m, 0.0)[..., None])
        l = p.sum(-1).reshape(n, hkvv, g)
        m = m.reshape(n, hkvv, g)
        o = jnp.einsum('bjs,bskd->bjkd', p.astype(bf16), vc, preferred_element_type=f32)
        o = jnp.where(eye, o.reshape(n, hkvv, g, hkvv, dh), 0.0).sum(3)
        mx = lax.pmax(m, 'sp')
        a = jnp.exp(m - mx)
        den = lax.psum(a * l, 'sp')
        num = lax.psum(a[..., None] * o, 'sp')
        out = (num / den[..., None]).astype(bf16).reshape(n, h * dh)
        rows = wo.shape[0]
        mine = lax.dynamic_slice_in_dim(out, me * rows, rows, axis=1)
        y = lax.psum(jnp.dot(mine, wo, preferred_element_type=f32), 'sp').astype(bf16)
        return y, kc, vc

    cache = P('dp', 'sp', None, None)
    return jax.shard_map(
        local, mesh=mesh,
        in_specs=(P('dp', None), P(None, None), P(None, None), P(None, None), P('sp', None),
                  cache, cache, P('dp'), P('dp')),
        out_specs=(P('dp', None), cache, cache),
        check_vma=False)
```

profile of v0, /device:TPU:97, one launch (start us, length us, event | category | flops | bytes accessed | tf_op | source)
XLA Modules:
  0.0 285.4 jit_solution(11564060630575881886)
XLA Ops:
  7.2 0.0 copy-start
  7.2 0.1 all-reduce.3.cloned.1.call-start
  7.3 0.7 copy-done
  8.0 0.0 copy-start.2
  8.0 8.2 %fusion.21 = bf16[1,4,8,128]{3,1,2,0:T(4,128)(2,1)S(1)} fusion(bf16[4,8192]{1,0:T(4,128)(2,1)S(1)} %copy-done, bf16[8192,1024]{1,0:T(8,128)(2,1)} %param.12), kind=kOutput, calls=%fused_computation.16 | convolution fusion | flops 67112960 | bytes 16850944 | tf_op jit(solution)/shard_map/dot_general | solution.py:19
  16.2 2.4 copy-done.2
  18.6 2.3 fusion.20
  20.8 0.1 broadcast_in_dim.97
  20.9 0.1 broadcast_in_dim.98
  21.0 0.0 copy-start.4
  21.0 0.0 copy-start.5
  21.0 43.5 %fusion.19 = bf16[1,4,64,128]{3,1,2,0:T(4,128)(2,1)S(1)} fusion(bf16[4,8192]{1,0:T(4,128)(2,1)S(1)} %copy-done, bf16[8192,8192]{1,0:T(8,128)(2,1)} %param.10), kind=kOutput, calls=%fused_computation.12 | convolution fusion | flops 536903680 | bytes 134348800 | tf_op jit(solution)/shard_map/dot_general | solution.py:17
  64.6 0.0 copy-done.4
  64.6 0.0 copy-done.5
  64.6 0.1 broadcast_compare_fusion.1
  64.7 13.4 %broadcast_select_fusion.1 = (bf16[4,1024,8,128]{3,2,1,0:T(8,128)(2,1)S(1)}, bf16[4,1024,8,128]{3,2,1,0:T(8,128)(2,1)}) fusion(bf16[4,1024,8,128]{3,2,1,0:T(8,128)(2,1)} %param.14, pred[4,1024]{1,0:T(4,128)(4,1)S(1)} %get-tuple-element.6, bf16[4,8,128]{2,1,0:T(8,128)(2,1)S(1)} %get-tuple-element.12, bf16[4,1024,8,128]{3,2,1,0:T(8,128)(2,1)} %param.15, ...), kind=kLoop, calls=%fused_computation.6 | loop fusion | flops 8388608 | bytes 33574912 | tf_op jit(solution)/shard_map/jit(_where)/select_n | solution.py:23
  78.1 0.0 copy-start.3
  78.1 2.8 fusion.37
  80.9 0.6 copy-done.3
  81.5 0.1 reshape.89
  81.6 0.3 fusion.22
  81.9 0.0 copy-start.1
  81.9 5.1 %fusion.16 = f32[4,64,128]{2,1,0:T(8,128)S(1)} fusion(bf16[4,1024,8,128]{3,2,1,0:T(8,128)(2,1)} %get-tuple-element.8, f32[4,64,1024]{2,1,0:T(8,128)S(1)} %get-tuple-element.10, f32[4,64]{1,0:T(4,128)S(1)} %is-finite_select_fusion, pred[64,8]{0,1:T(8,128)(4,1)S(1)} %broadcast_in_dim.98), kind=kOutput, calls=%fused_computation.11 | convolution fusion | flops 537886720 | bytes 9569792 | tf_op jit(solution)/shard_map/bjs,bskd->bjkd/dot_general | solution.py:34
  87.0 0.1 reshape.90
  87.1 49.8 %pmax.7 = f32[4,8,8]{2,1,0:T(8,128)S(1)} all-reduce(f32[4,8,8]{2,1,0:T(8,128)S(1)} %reshape.89), channel_id=1, replica_groups=mesh['dp'=1,'sp'=32] {'sp'}, use_global_device_ids=true, to_apply=%region_1.2 | all-reduce | flops 256 | bytes 2048 | tf_op jit(solution)/shard_map/pmax | solution.py:36
  136.9 0.8 bitcast_multiply_fusion
  137.7 0.1 all-reduce.3.cloned.1.call-update
  137.8 43.7 %psum.22 = f32[4,8,8]{2,1,0:T(8,128)S(1)} all-reduce(f32[4,8,8]{2,1,0:T(8,128)S(1)} %get-tuple-element.3), channel_id=1, replica_groups=mesh['dp'=1,'sp'=32] {'sp'}, use_global_device_ids=true, to_apply=%region_5.6 | all-reduce | flops 256 | bytes 2048 | tf_op jit(solution)/shard_map/psum | solution.py:38
  181.5 46.9 %all-reduce.3.cloned.1.call-done = f32[4,8,8,128]{3,2,1,0:T(8,128)} async-done(((f32[4,8,8,128]{3,2,1,0:T(8,128)}), f32[4,8,8,128]{3,2,1,0:T(8,128)}) %all-reduce.3.cloned.1.call-update) | async-done | bytes 131088 | tf_op jit(solution)/shard_map/psum | solution.py:39
  228.4 1.0 fusion.31
  229.4 0.1 copy.40
  229.4 2.8 fusion.32
  232.3 46.2 %all-reduce.4 = bf16[4,8192]{1,0:T(4,128)(2,1)} all-reduce(f32[4,8192]{1,0:T(4,128)S(1)} %fusion.32), channel_id=1, replica_groups=mesh['dp'=1,'sp'=32] {'sp'}, use_global_device_ids=true, to_apply=%region_6.7 | all-reduce | flops 32768 | bytes 196608 | tf_op jit(solution)/shard_map/psum | solution.py:43
  278.5 0.0 copy-done.1
  (6 shorter events, 0.0 us)
Async XLA Ops:
  7.2 0.8 copy-start
  7.2 221.2 %all-reduce.3.cloned.1.call-start = ((), (), s32[]{:S(2)}) async-start(), calls=%async_computation | async-start | bytes 262144 | tf_op jit(solution)/shard_map/psum | solution.py:39
  8.0 10.5 %copy-start.2 = (bf16[8192,1024]{1,0:T(8,128)(2,1)S(1)}, bf16[8192,1024]{1,0:T(8,128)(2,1)}, u32[]{:S(2)}) copy-start(bf16[8192,1024]{1,0:T(8,128)(2,1)} %param.11) | copy-start | bytes 50331652
  21.0 43.6 %copy-start.4 = (s32[4]{0:T(128)S(1)}, s32[4]{0:T(128)}, u32[]{:S(2)}) copy-start(s32[4]{0:T(128)} %param.17) | copy-start | bytes 52
  21.0 43.6 %copy-start.5 = (s32[4]{0:T(128)S(1)}, s32[4]{0:T(128)}, u32[]{:S(2)}) copy-start(s32[4]{0:T(128)} %param.16) | copy-start | bytes 52
  78.1 3.4 %copy-start.3 = (bf16[4,1024,8,128]{3,2,1,0:T(8,128)(2,1)}, bf16[4,1024,8,128]{3,2,1,0:T(8,128)(2,1)S(1)}, u32[]{:S(2)}) copy-start(bf16[4,1024,8,128]{3,2,1,0:T(8,128)(2,1)S(1)} %get-tuple-element.7) | copy-start | bytes 25165828
  81.9 196.6 %copy-start.1 = (bf16[4,8192]{1,0:T(4,128)(2,1)S(1)}, bf16[4,8192]{1,0:T(4,128)(2,1)}, u32[]{:S(2)}) copy-start(bf16[4,8192]{1,0:T(4,128)(2,1)} %param.9) | copy-start | bytes 196612
Sparse Core Ops, SparseCore 0:
  137.9 90.4 all-reduce.2
where the time goes:
time: 286 us; the launch traced here: 285 us
  blocking collectives  140 us (49%)
  matrix products  64.6 us (23%)
  waiting for transfers between devices  46.9 us (16%)
  other arithmetic  15.6 us (5%)
  between operations  14.2 us (5%)
  local copies, waits for them, and re-layouts  4.15 us (1%)
    pmax x1, blocking collectives, local(): mx = lax.pmax(m, 'sp')  49.8 us
    psum x1, waiting for transfers between devices, local(): num = lax.psum(a[..., None] * o, 'sp')  46.9 us
    psum x1, blocking collectives, local(): lax.psum(jnp.dot(mine, wo, preferred_element_type=f32), 'sp').astype(bf16)  46.2 us
    psum x1, blocking collectives, local(): den = lax.psum(a * l, 'sp')  43.7 us
    dot_general x1, matrix products, local(): jnp.dot(x, wq, preferred_element_type=f32).astype(bf16)  43.5 us
    select_n x1, other arithmetic, local(): kc = jnp.where(hit, k, kc)  13.4 us
    dot_general x1, matrix products, local(): jnp.dot(x, wv, preferred_element_type=f32).astype(bf16)  8.18 us
  transfers between devices with their start and end apart: 1, of which 1 were waited for; matrix products, arithmetic and copies ran while one was open for 0% of the time, Pallas kernels for 0%

commit v1 on v0

v1 whole, which is shorter than its diff:
```python
import functools
import jax
import jax.numpy as jnp
from jax import lax
from jax.experimental import pallas as pl
from jax.experimental.pallas import tpu as pltpu
from jax.sharding import PartitionSpec as P

MESH = pl.DeviceIdType.MESH
F32 = jnp.float32
BF16 = jnp.bfloat16
NQ = 4
R = 16


def peer(n, k):
    return lax.rem(lax.axis_index('sp') + k, n)


def barrier(n):
    sem = pltpu.get_barrier_semaphore()

    def one(k, c):
        pl.semaphore_signal(sem, 1, device_id={'sp': peer(n, k)}, device_id_type=MESH)
        return c
    lax.fori_loop(1, n, one, 0)
    return sem


def far_first(n):
    return sorted(range(1, n), key=lambda k: (-min(k, n - k), k))


def all_of(refs, sem):
    pltpu.make_async_copy(refs, refs, sem).wait()


def project(n, x, wq, wk, wv, kc, vc, qall, kvn, kv, vv,
            wqb, wkvb, qs, kvs, part, theirs, wsem, csem, ps, pr, qss, qrs, kss, krs):
    me = lax.axis_index('sp')
    d = x.shape[1]
    nb = x.shape[0]
    cols = wqb.shape[1]
    half = wkvb.shape[0]
    r = lax.rem(me, 2)
    t = lax.div(me, 2)
    heads = wk.shape[1] // 128
    bar = barrier(n)
    row0 = pl.multiple_of(r * half, half)

    @pl.when(t < heads)
    def _():
        pltpu.make_async_copy(wk.at[pl.ds(row0, half), pl.ds(pl.multiple_of(t * 128, 128), 128)], wkvb, wsem.at[NQ]).start()

    @pl.when(t >= heads)
    def _():
        pltpu.make_async_copy(wv.at[pl.ds(row0, half), pl.ds(pl.multiple_of((t - heads) * 128, 128), 128)], wkvb, wsem.at[NQ]).start()
    step = d // NQ
    wcp = [pltpu.make_async_copy(wq.at[pl.ds(i * step, step), pl.ds(pl.multiple_of(me * cols, cols), cols)],
                                 wqb.at[pl.ds(i * step, step)], wsem.at[i]) for i in range(NQ)]
    for c in wcp:
        c.start()
    ccp = [pltpu.make_async_copy(kc, kv, csem.at[0]), pltpu.make_async_copy(vc, vv, csem.at[1])]
    for c in ccp:
        c.start()
    pltpu.make_async_copy(wk.at[pl.ds(0, half), pl.ds(0, 128)], wkvb, wsem.at[NQ]).wait()
    kvp = jnp.dot(x[:, pl.ds(row0, half)], wkvb[...], preferred_element_type=F32)
    part[...] = jnp.concatenate([kvp, kvp], axis=0)
    pl.semaphore_wait(bar, n - 1)
    swap = pltpu.make_async_remote_copy(part, theirs, ps, pr, device_id={'sp': me + 1 - 2 * r}, device_id_type=MESH)
    q = jnp.zeros((nb, cols), F32)
    for i in range(NQ):
        wcp[i].wait()
        q = q + jnp.dot(x[:, i * step:(i + 1) * step], wqb[i * step:(i + 1) * step], preferred_element_type=F32)
        if i == 0:
            swap.start()
    qs[...] = jnp.concatenate([q[:, :128], q[:, 128:]], axis=0).astype(BF16)
    qall[me] = qs[...]
    swap.wait()
    kvs[...] = (part[...] + theirs[...]).astype(BF16)
    kvn[t] = kvs[...]

    def sendq(k, c):
        pltpu.make_async_remote_copy(qs, qall.at[me], qss, qrs, device_id={'sp': peer(n, k)}, device_id_type=MESH).start()
        return c
    lax.fori_loop(1, n, sendq, 0)

    def sendkv(k, c):
        pltpu.make_async_remote_copy(kvs, kvn.at[t], kss, krs, device_id={'sp': peer(n, 2 * k)}, device_id_type=MESH).start()
        return c
    lax.fori_loop(1, n // 2, sendkv, 0)
    all_of(qall.at[pl.ds(0, n - 1)], qss)
    all_of(kvn.at[pl.ds(0, n // 2 - 1)], kss)
    all_of(qall.at[pl.ds(0, n - 1)], qrs)
    all_of(kvn.at[pl.ds(0, n // 2 - 1)], krs)
    for c in ccp:
        c.wait()


def attend(n, pos, qall, kvn, kv, vv, ko, vo, om, qb, s_ref, ob, gb, rw, wsem, rsem):
    me = lax.axis_index('sp')
    nb, rows, dh = kv.shape
    hk = 8
    sl = rows // hk
    nh = 2 * n
    start = me * sl
    cp = []
    for b in range(nb):
        cp.append((pltpu.make_async_copy(kv.at[b], ko.at[b], wsem.at[0, b]),
                   pltpu.make_async_copy(vv.at[b], vo.at[b], wsem.at[1, b])))
    for c in cp:
        c[0].start()
        c[1].start()
    m_ = nb * nh
    i0 = lax.broadcasted_iota(jnp.int32, (m_, m_), 0)
    i1 = lax.broadcasted_iota(jnp.int32, (m_, m_), 1)
    want = (lax.rem(i0, nh) // 2) * (2 * nb) + lax.rem(i0, 2) * nb + i0 // nh
    perm = (i1 == want).astype(F32).astype(BF16)
    qb[...] = jnp.dot(perm, qall[...].reshape(m_, dh), preferred_element_type=F32).astype(BF16)
    nt = kvn.shape[0]
    j0 = lax.broadcasted_iota(jnp.int32, (nt * nb, nt * 2 * nb), 0)
    j1 = lax.broadcasted_iota(jnp.int32, (nt * nb, nt * 2 * nb), 1)
    want2 = ((j0 // (nb * hk)) * hk + lax.rem(j0, hk)) * 2 * nb + lax.rem(j0 // hk, nb)
    perm2 = (j1 == want2).astype(F32).astype(BF16)
    rw[...] = jnp.dot(perm2, kvn[...].reshape(nt * 2 * nb, dh), preferred_element_type=F32).astype(BF16).reshape(2 * nb, hk, dh)
    ch = 1024
    row = lax.broadcasted_iota(jnp.int32, (nh, ch), 0) // hk
    lane = lax.broadcasted_iota(jnp.int32, (nh, ch), 1)
    diag = row == lax.rem(lane, hk)
    glane = lax.broadcasted_iota(jnp.int32, (nh, dh), 1)
    ghalf = lax.rem(lax.broadcasted_iota(jnp.int32, (nh, dh), 0), 2)
    g = jnp.zeros((nh, dh), F32)
    c = dh ** -0.5
    for b in range(nb):
        lim = (pos[b] - start) * hk
        q = qb[b * nh:(b + 1) * nh]
        mx = jnp.full((nh, 1), -jnp.inf, F32)
        for i in range(rows // ch):
            s = lax.dot_general(q, kv[b, i * ch:(i + 1) * ch], (((1,), (1,)), ((), ())), preferred_element_type=F32) * c
            s = jnp.where(diag & (lane < lim - i * ch), s, -jnp.inf)
            mx = jnp.maximum(mx, s.max(1, keepdims=True))
            s_ref[:, i * ch:(i + 1) * ch] = s
        safe = jnp.where(mx == -jnp.inf, 0.0, mx)
        l = jnp.zeros((nh, 1), F32)
        o = jnp.zeros((nh, dh), F32)
        for i in range(rows // ch):
            p = jnp.exp(s_ref[:, i * ch:(i + 1) * ch] - safe)
            l = l + p.sum(1, keepdims=True)
            o = o + jnp.dot(p.astype(BF16), vv[b, i * ch:(i + 1) * ch], preferred_element_type=F32)
        ob[...] = o
        for h in range(2):
            om[pl.ds(h * nb + b, n, stride=R), :] = ob[pl.ds(h, n, stride=2), :]
        g = g + jnp.where(glane == ghalf * nb + b, mx, 0.0) + jnp.where(glane == 2 * nb + ghalf * nb + b, l, 0.0)
    gb[...] = g
    stat = gb[pl.ds(0, n, stride=2), :]
    stat2 = gb[pl.ds(1, n, stride=2), :]
    gl = lax.rem(lax.broadcasted_iota(jnp.int32, (n, dh), 1), 2 * nb)
    om[pl.ds(2 * nb, n, stride=R), :] = jnp.where(gl < nb, stat, stat2)
    for b in range(nb):
        cp[b][0].wait()
        cp[b][1].wait()
    for b in range(nb):
        at = pos[b] - start

        @pl.when((at >= 0) & (at < sl))
        def _():
            k1 = pltpu.make_async_copy(rw.at[b], ko.at[b, pl.ds(at * hk, hk)], rsem.at[0])
            k2 = pltpu.make_async_copy(rw.at[nb + b], vo.at[b, pl.ds(at * hk, hk)], rsem.at[1])
            k1.start()
            k2.start()
            k1.wait()
            k2.wait()


def finish(n, qall, kvn, om, wo, yo, wob, orx, ys, yrx, yb, wsem, os_, or_, ys_, yr_, gs_, gr_):
    me = lax.axis_index('sp')
    dh = qall.shape[2]
    hk = kvn.shape[0] // 2
    nb = 4
    cols = wo.shape[1] // n
    bar = barrier(n)
    wcp = pltpu.make_async_copy(wo, wob, wsem)
    wcp.start()
    pl.semaphore_wait(bar, n - 1)

    def slot(i, r):
        return pl.ds(pl.multiple_of(i * r, r), r)

    def sendo(k, c):
        to = peer(n, k)
        pltpu.make_async_remote_copy(om.at[slot(to, R)], orx.at[slot(me, R)], os_, or_,
                                     device_id={'sp': to}, device_id_type=MESH).start()
        return c
    lax.fori_loop(1, n, sendo, 0)
    orx[slot(me, R), :] = om[slot(me, R), :]
    kh = lax.div(me * hk, n)
    knew = kvn[kh].astype(F32)
    vnew = kvn[hk + kh].astype(F32)
    snew = (qall[me].astype(F32) * knew).sum(1, keepdims=True) * dh ** -0.5
    all_of(om.at[pl.ds(0, (n - 1) * R)], os_)
    all_of(orx.at[pl.ds(0, (n - 1) * R)], or_)
    st = orx[pl.ds(2 * nb, n, stride=R), :].T
    m = st[0:2 * nb]
    l = st[2 * nb:4 * nb]
    top = jnp.maximum(m.max(1, keepdims=True), snew)
    a = jnp.exp(m - top)
    anew = jnp.exp(snew - top)
    den = (a * l).sum(1, keepdims=True) + anew
    num = anew * vnew
    for i in range(n):
        num = num + a[:, i:i + 1] * orx[i * R:i * R + 2 * nb, :]
    o = (num / den)
    o = jnp.concatenate([o[:nb], o[nb:]], axis=1).astype(BF16)
    wcp.wait()
    order = far_first(n) + [0]
    for g in range(0, n, 8):
        for k in order[g:g + 8]:
            to = peer(n, k)
            w = wob[:, pl.ds(pl.multiple_of(to * cols, cols), cols)]
            part = jnp.dot(o, w, preferred_element_type=F32)
            part = jnp.concatenate([part[:, :128], part[:, 128:]], axis=0)
            if k:
                ys[to] = part
            else:
                yrx[me] = part
        for k in order[g:g + 8]:
            if k:
                to = peer(n, k)
                pltpu.make_async_remote_copy(ys.at[to], yrx.at[me], ys_, yr_, device_id={'sp': to}, device_id_type=MESH).start()
    all_of(ys.at[pl.ds(0, n - 1)], ys_)
    all_of(yrx.at[pl.ds(0, n - 1)], yr_)
    yb[...] = yrx[...].sum(0).astype(BF16)
    yo[me] = yb[...]

    def sendy(k, c):
        to = peer(n, k)
        pltpu.make_async_remote_copy(yb, yo.at[me], gs_, gr_, device_id={'sp': to}, device_id_type=MESH).start()
        return c
    lax.fori_loop(1, n, sendy, 0)
    all_of(yo.at[pl.ds(0, n - 1)], gs_)
    all_of(yo.at[pl.ds(0, n - 1)], gr_)


def solution(mesh):
    n = mesh.shape['sp']
    vm = pl.BlockSpec(memory_space=pltpu.VMEM)
    hbm = pl.BlockSpec(memory_space=pltpu.HBM)
    sm = pl.BlockSpec(memory_space=pltpu.SMEM)
    dma = pltpu.SemaphoreType.DMA

    def params(i, mib):
        return pltpu.CompilerParams(collective_id=i, has_side_effects=i is not None, vmem_limit_bytes=mib * 2**20)

    def local(x, wq, wk, wv, wo, kc, vc, pos, lens):
        nb, d = x.shape
        _, sl, hk, dh = kc.shape
        cols = wq.shape[1] // n
        nt = 2 * hk
        half = d * nt // n
        kc = kc.reshape(nb, sl * hk, dh)
        vc = vc.reshape(nb, sl * hk, dh)
        shape = kc.shape
        wq, wk, wv, wo, kc, vc = (pltpu.with_memory_space_constraint(a, pltpu.HBM) for a in (wq, wk, wv, wo, kc, vc))
        qall, kvn, kv, vv = pl.pallas_call(
            functools.partial(project, n),
            out_shape=[pltpu.VMEM((n, 2 * nb, dh), BF16), pltpu.VMEM((nt, 2 * nb, dh), BF16),
                       pltpu.VMEM(shape, BF16), pltpu.VMEM(shape, BF16)],
            in_specs=[vm, hbm, hbm, hbm, hbm, hbm], out_specs=[vm] * 4,
            scratch_shapes=[pltpu.VMEM((d, cols), BF16), pltpu.VMEM((half, dh), BF16),
                            pltpu.VMEM((2 * nb, dh), BF16), pltpu.VMEM((2 * nb, dh), BF16),
                            pltpu.VMEM((2 * nb, dh), F32), pltpu.VMEM((2 * nb, dh), F32),
                            dma((NQ + 1,)), dma((2,))] + [dma] * 6,
            compiler_params=params(0, 16), name='project')(x, wq, wk, wv, kc, vc)
        ko, vo, om = pl.pallas_call(
            functools.partial(attend, n),
            out_shape=[jax.ShapeDtypeStruct(shape, BF16), jax.ShapeDtypeStruct(shape, BF16), pltpu.VMEM((n * R, dh), F32)],
            in_specs=[sm, vm, vm, vm, vm], out_specs=[hbm, hbm, vm],
            scratch_shapes=[pltpu.VMEM((n * 2 * nb, dh), BF16), pltpu.VMEM((2 * n, sl * hk), F32),
                            pltpu.VMEM((2 * n, dh), F32), pltpu.VMEM((2 * n, dh), F32), pltpu.VMEM((2 * nb, hk, dh), BF16),
                            dma((2, nb)), dma((2,))],
            compiler_params=params(None, 16), name='attend')(pos, qall, kvn, kv, vv)
        y = pl.pallas_call(
            functools.partial(finish, n),
            out_shape=jax.ShapeDtypeStruct((n, 2 * nb, dh), BF16),
            in_specs=[vm, vm, vm, hbm], out_specs=vm,
            scratch_shapes=[pltpu.VMEM(wo.shape, BF16), pltpu.VMEM((n * R, dh), F32), pltpu.VMEM((n, 2 * nb, dh), F32),
                            pltpu.VMEM((n, 2 * nb, dh), F32), pltpu.VMEM((2 * nb, dh), BF16)] + [dma] * 7,
            compiler_params=params(1, 16), name='finish')(qall, kvn, om, wo)
        y = y.reshape(n, 2, nb, dh).transpose(2, 0, 1, 3).reshape(nb, -1)
        return y, ko.reshape(nb, sl, hk, dh), vo.reshape(nb, sl, hk, dh)

    cache = P('dp', 'sp', None, None)
    return jax.shard_map(
        local, mesh=mesh,
        in_specs=(P('dp', None), P(None, None), P(None, None), P(None, None), P('sp', None),
                  cache, cache, P('dp'), P('dp')),
        out_specs=(P('dp', None), cache, cache),
        check_vma=False)
```

time: 286 us -> 49.6 us (0.17)
  blocking collectives: 140 us -> 0 us
  matrix products: 64.6 us -> 0 us
  Pallas kernels: 0 us -> 47.4 us
  waiting for transfers between devices: 46.9 us -> 0 us
  other arithmetic: 15.6 us -> 0 us
  between operations: 14.2 us -> 0.67 us
    psum x2 -> x0, blocking collectives: 90 us -> none  [the longest x1 46.2 us: local(): lax.psum(jnp.dot(mine, wo, preferred_element_type=f32), 'sp').astype(bf16)]
    dot_general x6 -> x0, matrix products: 64.6 us -> none  [the longest x1 43.5 us: local(): jnp.dot(x, wq, preferred_element_type=f32).astype(bf16)]
    pmax x1 -> x0, blocking collectives: 49.8 us -> none  [local(): mx = lax.pmax(m, 'sp')]
    pallas_call x0 -> x3, Pallas kernels: none -> 47.4 us  [the longest x1 21.7 us: local(): pl.pallas_call(functools.partial(finish, n), out_shape=jax.ShapeDtypeStru...]
    psum x1 -> x0, waiting for transfers between devices: 46.9 us -> none  [local(): num = lax.psum(a[..., None] * o, 'sp')]
    select_n x2 -> x0, other arithmetic: 13.4 us -> none  [the longest x1 13.4 us: local(): kc = jnp.where(hit, k, kc)]
  transfers between devices with their start and end apart: 1 -> 0, of which waited for: 1 -> 0; matrix products, arithmetic and copies ran while one was open for 0% -> 0% of each run, Pallas kernels for 0% -> 0%
where the time goes in v1:
time: 49.6 us; the launch traced here: 49.5 us
  Pallas kernels  47.4 us (96%)
  local copies, waits for them, and re-layouts  1.47 us (3%)
  between operations  0.67 us (1%)
    pallas_call x1, Pallas kernels, local(): pl.pallas_call(functools.partial(finish, n), out_shape=jax.ShapeDtypeStru...  21.7 us
    pallas_call x1, Pallas kernels, local(): pl.pallas_call(functools.partial(project, n), out_shape=[pltpu.VMEM((n, 2...  16.1 us
    pallas_call x1, Pallas kernels, local(): pl.pallas_call(functools.partial(attend, n), out_shape=[jax.ShapeDtypeStr...  9.58 us
    unnamed x5, local copies, waits for them, and re-layouts  1.47 us

profile of v1, /device:TPU:97, one launch (start us, length us, event | category | flops | bytes accessed | tf_op | source)
XLA Modules:
  0.0 49.5 jit_solution(6062508717965754663)
XLA Ops:
  0.6 0.0 copy-start
  0.6 0.8 %copy-done = bf16[4,8192]{1,0:T(4,128)(2,1)S(1)} copy-done((bf16[4,8192]{1,0:T(4,128)(2,1)S(1)}, bf16[4,8192]{1,0:T(4,128)(2,1)}, u32[]{:S(2)}) %copy-start) | copy-done | bytes 65560
  1.5 0.0 copy-start.1
  1.5 16.1 %project.1 = (bf16[32,8,128]{2,1,0:T(8,128)(2,1)S(1)}, bf16[16,8,128]{2,1,0:T(8,128)(2,1)S(1)}, bf16[4,8192,128]{2,1,0:T(8,128)(2,1)S(1)}, bf16[4,8192,128]{2,1,0:T(8,128)(2,1)S(1)}) custom-call(bf16[4,8192]{1,0:T(4,128)(2,1)S(1)} %copy-done, bf16[8192,8192]{1,0:T(8,128)(2,1)} %wq.1, bf16[8192,1024]{1,0:T(8,128)(2,1)} %wk.1, bf16[8192,1024]{1,0:T(8,128)(2,1)} %wv.1, ...), custom_call_target="tpu_custom_call" | custom-call | tf_op jit(solution)/shard_map/project/pallas_call | solution.py:264
  17.6 0.0 copy-done.1
  17.6 9.6 %attend.1 = (bf16[4,8192,128]{2,1,0:T(8,128)(2,1)}, bf16[4,8192,128]{2,1,0:T(8,128)(2,1)}, f32[512,128]{1,0:T(8,128)S(1)}) custom-call(s32[4]{0:T(128)S(1)} %copy-done.1, bf16[32,8,128]{2,1,0:T(8,128)(2,1)S(1)} %get-tuple-element.10.qall, bf16[16,8,128]{2,1,0:T(8,128)(2,1)S(1)} %get-tuple-element.11.kvn, bf16[4,8192,128]{2,1,0:T(8,128)(2,1)S(1)} %get-tuple-element.12.kv, ...), custom_call_target="tpu_custom_call" | custom-call | tf_op jit(solution)/shard_map/attend/pallas_call | solution.py:274
  27.2 21.7 %finish.1 = bf16[32,8,128]{2,1,0:T(8,128)(2,1)S(1)} custom-call(bf16[32,8,128]{2,1,0:T(8,128)(2,1)S(1)} %get-tuple-element.10.qall, bf16[16,8,128]{2,1,0:T(8,128)(2,1)S(1)} %get-tuple-element.11.kvn, f32[512,128]{1,0:T(8,128)S(1)} %get-tuple-element.14.om, bf16[256,8192]{1,0:T(8,128)(2,1)} %wo.1), custom_call_target="tpu_custom_call" | custom-call | tf_op jit(solution)/shard_map/finish/pallas_call | solution.py:282
  48.9 0.6 %copy.13 = bf16[4,8192]{1,0:T(4,128)(2,1)} copy(bf16[4,8192]{1,0:T(4,128)(2,1)S(1)} %bitcast.9) | data formatting | bytes 131072
Async XLA Ops:
  0.6 0.8 %copy-start = (bf16[4,8192]{1,0:T(4,128)(2,1)S(1)}, bf16[4,8192]{1,0:T(4,128)(2,1)}, u32[]{:S(2)}) copy-start(bf16[4,8192]{1,0:T(4,128)(2,1)} %x.1) | copy-start | bytes 196612
  1.5 16.1 %copy-start.1 = (s32[4]{0:T(128)S(1)}, s32[4]{0:T(128)}, u32[]{:S(2)}) copy-start(s32[4]{0:T(128)} %pos.1) | copy-start | bytes 52

commit v2 on v0

v2 whole, which is shorter than its diff:
```python
import functools
import math
import jax
import jax.numpy as jnp
from jax import lax
from jax.experimental import pallas as pl
from jax.experimental.pallas import tpu as pltpu
from jax.sharding import PartitionSpec as P

MESH = pl.DeviceIdType.MESH
F32 = jnp.float32
BF16 = jnp.bfloat16
NQ = 8
CT = 1024
CH = 512
R = 9


def peer(n, k):
    return lax.rem(lax.axis_index('sp') + k, n)


def far_first(n, ks):
    side = max(1, math.isqrt(n // 2))

    def hops(k):
        a, b = (k // 2) % side, (k // 2) // side
        return min(a, side - a) + min(b, side - b)
    return sorted(ks, key=lambda k: (-hops(k), k))


def barrier(n):
    sem = pltpu.get_barrier_semaphore()
    for k in far_first(n, range(1, n)):
        pl.semaphore_signal(sem, 1, device_id={'sp': peer(n, k)}, device_id_type=MESH)
    return sem


def all_of(refs, sem):
    pltpu.make_async_copy(refs, refs, sem).wait()


class Softmax:
    def __init__(self, q2, kt, vb, lim, s_ref, hk):
        nh, dh = q2.shape[0] // 2, q2.shape[1] // 2
        self.nh, self.dh, self.kt, self.vb, self.lim, self.s = nh, dh, kt, vb, lim, s_ref
        self.c2 = dh ** -0.5 * math.log2(math.e)
        self.q2 = q2
        row = lax.broadcasted_iota(jnp.int32, (nh, 128), 0) // hk
        self.lane = lax.broadcasted_iota(jnp.int32, (nh, 128), 1)
        self.bias = jnp.where(row == lax.rem(self.lane, hk), 0.0, -jnp.inf)
        self.mx = jnp.full((nh, 128), -jnp.inf, F32)
        self.l = jnp.zeros((nh, 128), F32)
        self.o = jnp.zeros((2 * nh, 2 * dh), F32)

    def scores(self, i):
        nh, half = self.nh, CH // 2
        k2 = jnp.concatenate([self.kt[:, i:i + half], self.kt[:, i + half:i + CH]], axis=0)
        s = jnp.dot(self.q2[...], k2, preferred_element_type=F32)
        for u in range(2):
            for e in range(0, half, 128):
                se = jnp.where(self.lane < self.lim - (i + u * half + e), s[u * nh:(u + 1) * nh, e:e + 128] + self.bias, -jnp.inf)
                self.mx = jnp.maximum(self.mx, se)
                self.s[u * nh:(u + 1) * nh, i // 2 + e:i // 2 + e + 128] = se

    def maximum(self):
        self.m = self.mx.max(1, keepdims=True) * self.c2
        self.safe = jnp.where(self.m == -jnp.inf, 0.0, self.m)

    def values(self, i):
        nh, half = self.nh, CH // 2
        ps = []
        for u in range(2):
            row = []
            for e in range(0, half, 128):
                p = jnp.exp2(self.s[u * nh:(u + 1) * nh, i // 2 + e:i // 2 + e + 128] * self.c2 - self.safe)
                self.l = self.l + p
                row.append(p.astype(BF16))
            ps.append(jnp.concatenate(row, axis=1))
        v2 = jnp.concatenate([self.vb[i:i + half], self.vb[i + half:i + CH]], axis=1)
        self.o = self.o + jnp.dot(jnp.concatenate(ps, axis=0), v2, preferred_element_type=F32)

    def result(self):
        nh, dh = self.nh, self.dh
        return self.m, self.l.sum(1, keepdims=True), self.o[:nh, :dh] + self.o[nh:, dh:]


def put(n, nb, b, m, l, o, om, ob):
    nh, dh = o.shape
    ob[...] = o
    for h in range(2):
        om[:, h * nb + b, :] = ob[pl.ds(h, n, stride=2), :]
    glane = lax.broadcasted_iota(jnp.int32, (nh, dh), 1)
    at = lax.rem(lax.broadcasted_iota(jnp.int32, (nh, dh), 0), 2) * nb + b
    return jnp.where(glane == at, m, 0.0) + jnp.where(glane == 2 * nb + at, l, 0.0)


def stats_row(n, g, gb):
    gb[...] = g
    return gb[pl.ds(0, n, stride=2), :] + gb[pl.ds(1, n, stride=2), :]


def decode(n, posh, x, wq, wk, wv, wo, kc, vc, yo, rw, kv, vv,
           qall, kvn, xb, wqb, wkvb, qs, kvs, part, theirs, perm_ref, q2, kt, s_ref, ob, gb, om, wob, orx, ys, yrx, yb,
           pos, psem, xsem, wsem, csem, osem, ps, pr, qss, qrs, kss, krs, os_, or_, ys_, yr_, gs_, gr_):
    me = lax.axis_index('sp')
    nb, d = x.shape
    cols = wqb.shape[1]
    half = wkvb.shape[0]
    r = lax.rem(me, 2)
    t = lax.div(me, 2)
    heads = wk.shape[1] // 128
    row0 = pl.multiple_of(r * half, half)
    xcp = pltpu.make_async_copy(x, xb, xsem)
    xcp.start()
    pcp = pltpu.make_async_copy(posh, pos, psem)
    pcp.start()

    @pl.when(t < heads)
    def _():
        pltpu.make_async_copy(wk.at[pl.ds(row0, half), pl.ds(pl.multiple_of(t * 128, 128), 128)], wkvb, wsem.at[NQ]).start()

    @pl.when(t >= heads)
    def _():
        pltpu.make_async_copy(wv.at[pl.ds(row0, half), pl.ds(pl.multiple_of((t - heads) * 128, 128), 128)], wkvb, wsem.at[NQ]).start()
    step = d // NQ
    wcp = [pltpu.make_async_copy(wq.at[pl.ds(i * step, step), pl.ds(pl.multiple_of(me * cols, cols), cols)],
                                 wqb.at[pl.ds(i * step, step)], wsem.at[i]) for i in range(NQ)]
    for c in wcp:
        c.start()
    bar = barrier(n)
    ccp = [pltpu.make_async_copy(f.at[b], t_.at[b], csem.at[e, b]) for e, (f, t_) in enumerate(((kc, kv), (vc, vv)))
           for b in range(nb)]
    xcp.wait()
    pcp.wait()
    pltpu.make_async_copy(wk.at[pl.ds(0, half), pl.ds(0, 128)], wkvb, wsem.at[NQ]).wait()
    kvp = jnp.dot(xb[:, pl.ds(row0, half)], wkvb[...], preferred_element_type=F32)
    part[...] = jnp.concatenate([kvp, kvp], axis=0)
    swap = pltpu.make_async_remote_copy(part, theirs, ps, pr, device_id={'sp': me + 1 - 2 * r}, device_id_type=MESH)
    q = jnp.zeros((nb, cols), F32)
    for i in range(NQ):
        wcp[i].wait()
        if i == NQ - 3:
            for c in ccp[:nb]:
                c.start()
        q = q + jnp.dot(xb[:, i * step:(i + 1) * step], wqb[i * step:(i + 1) * step], preferred_element_type=F32)
    qs[...] = jnp.concatenate([q[:, :128], q[:, 128:]], axis=0).astype(BF16)
    qall[me] = qs[...]
    pl.semaphore_wait(bar, n - 1)
    swap.start()

    for k in far_first(n, range(1, n)):
        pltpu.make_async_remote_copy(qs, qall.at[me], qss, qrs, device_id={'sp': peer(n, k)}, device_id_type=MESH).start()
    swap.wait()
    kvs[...] = (part[...] + theirs[...]).astype(BF16)
    kvn[t] = kvs[...]

    for k in far_first(n, range(2, n, 2)):
        pltpu.make_async_remote_copy(kvs, kvn.at[t], kss, krs, device_id={'sp': peer(n, k)}, device_id_type=MESH).start()
    wcp_o = pltpu.make_async_copy(wo, wob, osem)
    _, rows, dh = kv.shape
    hk = rw.shape[1]
    sl = rows // hk
    nh = 2 * n
    start = me * sl
    m_ = nb * nh
    i0 = lax.broadcasted_iota(jnp.int32, (m_, m_), 0)
    i1 = lax.broadcasted_iota(jnp.int32, (m_, m_), 1)
    want = (lax.rem(i0, nh) // 2) * (2 * nb) + lax.rem(i0, 2) * nb + i0 // nh
    perm_ref[...] = (i1 == want).astype(F32).astype(BF16)
    for b in range(nb):
        ccp[b].wait()
        ccp[nb + b].start()
        for i in range(0, kv.shape[1], CT):
            kt[b, :, i:i + CT] = kv[b, i:i + CT].T
    all_of(qall.at[pl.ds(0, n - 1)], qrs)
    wcp_o.start()
    qb = jnp.dot(perm_ref[...], qall[...].reshape(m_, dh), preferred_element_type=F32).astype(BF16)
    for b in range(nb):
        for u in range(2):
            q2[b, u * nh:(u + 1) * nh, u * dh:(u + 1) * dh] = qb[b * nh:(b + 1) * nh]
            q2[b, u * nh:(u + 1) * nh, (1 - u) * dh:(2 - u) * dh] = jnp.zeros((nh, dh), BF16)
    g = jnp.zeros((nh, dh), F32)
    at = [Softmax(q2.at[b], kt.at[b], vv.at[b], (pos[b] - start) * hk, s_ref.at[b % 2], hk) for b in range(nb)]
    for b in range(nb + 1):
        if b:
            ccp[nb + b - 1].wait()
        for i in range(0, rows, CH):
            if b < nb:
                at[b].scores(i)
            if b:
                at[b - 1].values(i)
        if b < nb:
            at[b].maximum()
        if b:
            g = g + put(n, nb, b - 1, *at[b - 1].result(), om, ob)
    om[:, 2 * nb, :] = stats_row(n, g, gb)
    cols = wo.shape[1] // n
    for k in far_first(n, range(1, n)):
        to = peer(n, k)
        pltpu.make_async_remote_copy(om.at[to], orx.at[me], os_, or_,
                                     device_id={'sp': to}, device_id_type=MESH).start()
    orx[me] = om[me]
    all_of(qall.at[pl.ds(0, n - 1)], qss)
    all_of(kvn.at[pl.ds(0, n // 2 - 1)], kss)
    all_of(kvn.at[pl.ds(0, n // 2 - 1)], krs)
    nt = kvn.shape[0]
    j0 = lax.broadcasted_iota(jnp.int32, (nt * nb, nt * 2 * nb), 0)
    j1 = lax.broadcasted_iota(jnp.int32, (nt * nb, nt * 2 * nb), 1)
    want2 = ((j0 // (nb * hk)) * hk + lax.rem(j0, hk)) * 2 * nb + lax.rem(j0 // hk, nb)
    perm2 = (j1 == want2).astype(F32).astype(BF16)
    rw[...] = jnp.dot(perm2, kvn[...].reshape(nt * 2 * nb, dh), preferred_element_type=F32).astype(BF16).reshape(2 * nb, hk, dh)
    kh = lax.div(me * hk, n)
    knew = kvn[kh].astype(F32)
    vnew = kvn[hk + kh].astype(F32)
    snew = (qall[me].astype(F32) * knew).sum(1, keepdims=True) * (dh ** -0.5 * math.log2(math.e))
    all_of(om.at[pl.ds(0, n - 1)], os_)
    all_of(orx.at[pl.ds(0, n - 1)], or_)
    st = orx[:, 2 * nb, :].T
    m = st[0:2 * nb]
    l = st[2 * nb:4 * nb]
    top = jnp.maximum(m.max(1, keepdims=True), snew)
    a = jnp.exp2(m - top)
    anew = jnp.exp2(snew - top)
    den = (a * l).sum(1, keepdims=True) + anew
    num = anew * vnew
    for i in range(n):
        num = num + a[:, i:i + 1] * orx[i, 0:2 * nb, :]
    o = (num / den)
    o = jnp.concatenate([o[:nb], o[nb:]], axis=1).astype(BF16)
    wcp_o.wait()
    order = far_first(n, range(n))
    for g in range(0, n, 8):
        for k in order[g:g + 8]:
            to = peer(n, k)
            w = wob[:, pl.ds(pl.multiple_of(to * cols, cols), cols)]
            part = jnp.dot(o, w, preferred_element_type=F32)
            part = jnp.concatenate([part[:, :128], part[:, 128:]], axis=0)
            if k:
                ys[to] = part
            else:
                yrx[me] = part
        for k in order[g:g + 8]:
            if k:
                to = peer(n, k)
                pltpu.make_async_remote_copy(ys.at[to], yrx.at[me], ys_, yr_, device_id={'sp': to}, device_id_type=MESH).start()
    all_of(ys.at[pl.ds(0, n - 1)], ys_)
    all_of(yrx.at[pl.ds(0, n - 1)], yr_)
    yb[...] = yrx[...].sum(0).astype(BF16)
    yo[me] = yb[...]

    for k in far_first(n, range(1, n)):
        pltpu.make_async_remote_copy(yb, yo.at[me], gs_, gr_, device_id={'sp': peer(n, k)}, device_id_type=MESH).start()
    all_of(yo.at[pl.ds(0, n - 1)], gs_)
    all_of(yo.at[pl.ds(0, n - 1)], gr_)


def store(n, pos, rw, y, kv, vv, ko, vo, yo, k2, v2, sem, ysem):
    nb, rows, _ = kv.shape
    hk = rw.shape[1]
    sl = rows // hk
    start = lax.axis_index('sp') * sl

    def bulk(b):
        return (pltpu.make_async_copy(k2.at[b], ko.at[b], sem.at[0, b]), pltpu.make_async_copy(v2.at[b], vo.at[b], sem.at[1, b]))

    def begin(b, own):
        at = pos[b] - start
        here = (at >= 0) & (at < sl)

        @pl.when(here if own else jnp.logical_not(here))
        def _():
            for a in bulk(b):
                a.start()
    for b in range(nb):
        at = pos[b] - start

        @pl.when((at >= 0) & (at < sl))
        def _():
            here = pl.ds(pl.multiple_of(at * hk, hk), hk)
            k2[b, here] = rw[b]
            v2[b, here] = rw[nb + b]
    for own in (False, True):
        for b in range(nb):
            begin(b, own)
    ycp = pltpu.make_async_copy(y, yo, ysem)
    ycp.start()
    ycp.wait()
    for b in range(nb):
        for a in bulk(b):
            a.wait()


def solution(mesh):
    n = mesh.shape['sp']
    vm = pl.BlockSpec(memory_space=pltpu.VMEM)
    hbm = pl.BlockSpec(memory_space=pltpu.HBM)
    sm = pl.BlockSpec(memory_space=pltpu.SMEM)
    dma = pltpu.SemaphoreType.DMA

    def params(i, mib):
        return pltpu.CompilerParams(collective_id=i, has_side_effects=i is not None, vmem_limit_bytes=mib * 2**20)

    def local(x, wq, wk, wv, wo, kc, vc, pos, lens):
        nb, d = x.shape
        _, sl, hk, dh = kc.shape
        cols = wq.shape[1] // n
        nt = 2 * hk
        half = d * nt // n
        kc = kc.reshape(nb, sl * hk, dh)
        vc = vc.reshape(nb, sl * hk, dh)
        shape = kc.shape
        x, wq, wk, wv, wo, kc, vc = (pltpu.with_memory_space_constraint(a, pltpu.HBM) for a in (x, wq, wk, wv, wo, kc, vc))
        small = (2 * nb, dh)
        y, rw, kv, vv = pl.pallas_call(
            functools.partial(decode, n),
            out_shape=[pltpu.VMEM((n,) + small, BF16), pltpu.VMEM((2 * nb, hk, dh), BF16), pltpu.VMEM(shape, BF16), pltpu.VMEM(shape, BF16)],
            in_specs=[hbm] * 8, out_specs=[vm] * 4,
            scratch_shapes=[pltpu.VMEM((n,) + small, BF16), pltpu.VMEM((nt,) + small, BF16),
                            pltpu.VMEM((nb, d), BF16), pltpu.VMEM((d, cols), BF16), pltpu.VMEM((half, dh), BF16),
                            pltpu.VMEM(small, BF16), pltpu.VMEM(small, BF16), pltpu.VMEM(small, F32), pltpu.VMEM(small, F32),
                            pltpu.VMEM((n * 2 * nb, n * 2 * nb), BF16), pltpu.VMEM((nb, 4 * n, 2 * dh), BF16), pltpu.VMEM((nb, dh, sl * hk), BF16), pltpu.VMEM((2, 4 * n, sl * hk // 2), F32),
                            pltpu.VMEM((2 * n, dh), F32), pltpu.VMEM((2 * n, dh), F32), pltpu.VMEM((n, R, dh), F32),
                            pltpu.VMEM(wo.shape, BF16), pltpu.VMEM((n, R, dh), F32), pltpu.VMEM((n,) + small, F32),
                            pltpu.VMEM((n,) + small, F32), pltpu.VMEM(small, BF16),
                            pltpu.SMEM((nb,), jnp.int32), dma, dma, dma((NQ + 1,)), dma((2, nb)), dma] + [dma] * 12,
            compiler_params=params(0, 36), name='decode')(pltpu.with_memory_space_constraint(pos, pltpu.HBM), x, wq, wk, wv, wo, kc, vc)
        ko, vo, y, _, _ = pl.pallas_call(
            functools.partial(store, n),
            out_shape=[jax.ShapeDtypeStruct(shape, BF16), jax.ShapeDtypeStruct(shape, BF16), jax.ShapeDtypeStruct(y.shape, BF16),
                       pltpu.VMEM(shape, BF16), pltpu.VMEM(shape, BF16)],
            in_specs=[sm, vm, vm, vm, vm], out_specs=[hbm, hbm, hbm, vm, vm],
            input_output_aliases={3: 3, 4: 4},
            scratch_shapes=[dma((2, nb)), dma],
            compiler_params=params(None, 4), name='store')(pos, rw, y, kv, vv)
        y = y.reshape(n, 2, nb, dh).transpose(2, 0, 1, 3).reshape(nb, -1)
        return y, ko.reshape(nb, sl, hk, dh), vo.reshape(nb, sl, hk, dh)

    cache = P('dp', 'sp', None, None)
    return jax.shard_map(
        local, mesh=mesh,
        in_specs=(P('dp', None), P(None, None), P(None, None), P(None, None), P('sp', None),
                  cache, cache, P('dp'), P('dp')),
        out_specs=(P('dp', None), cache, cache),
        check_vma=False)
```

time: 286 us -> 41.2 us (0.14)
  blocking collectives: 140 us -> 0 us
  matrix products: 64.6 us -> 0 us
  waiting for transfers between devices: 46.9 us -> 0 us
  Pallas kernels: 0 us -> 40.4 us
  other arithmetic: 15.6 us -> 0 us
  between operations: 14.2 us -> 0.66 us
  local copies, waits for them, and re-layouts: 4.15 us -> 0.01 us
    psum x2 -> x0, blocking collectives: 90 us -> none  [the longest x1 46.2 us: local(): lax.psum(jnp.dot(mine, wo, preferred_element_type=f32), 'sp').astype(bf16)]
    dot_general x6 -> x0, matrix products: 64.6 us -> none  [the longest x1 43.5 us: local(): jnp.dot(x, wq, preferred_element_type=f32).astype(bf16)]
    pmax x1 -> x0, blocking collectives: 49.8 us -> none  [local(): mx = lax.pmax(m, 'sp')]
    psum x1 -> x0, waiting for transfers between devices: 46.9 us -> none  [local(): num = lax.psum(a[..., None] * o, 'sp')]
    pallas_call x0 -> x2, Pallas kernels: none -> 40.4 us  [the longest x1 33.9 us: local(): pl.pallas_call(functools.partial(decode, n), out_shape=[pltpu.VMEM((n,) +...]
    select_n x2 -> x0, other arithmetic: 13.4 us -> none  [the longest x1 13.4 us: local(): kc = jnp.where(hit, k, kc)]
    unnamed x14 -> x2, local copies, waits for them, and re-layouts: 3.81 us -> 0.01 us
  transfers between devices with their start and end apart: 1 -> 0, of which waited for: 1 -> 0; matrix products, arithmetic and copies ran while one was open for 0% -> 0% of each run, Pallas kernels for 0% -> 0%
where the time goes in v2:
time: 41.2 us; the launch traced here: 41.1 us
  Pallas kernels  40.4 us (98%)
  between operations  0.66 us (2%)
    pallas_call x1, Pallas kernels, local(): pl.pallas_call(functools.partial(decode, n), out_shape=[pltpu.VMEM((n,) +...  33.9 us
    pallas_call x1, Pallas kernels, local(): pl.pallas_call(functools.partial(store, n), out_shape=[jax.ShapeDtypeStru...  6.54 us

profile of v2, /device:TPU:97, one launch (start us, length us, event | category | flops | bytes accessed | tf_op | source)
XLA Modules:
  0.0 41.1 jit_solution(2907526735796143437)
XLA Ops:
  0.6 0.0 copy-start
  0.6 33.9 %decode.1 = (bf16[32,8,128]{2,1,0:T(8,128)(2,1)S(1)}, bf16[8,8,128]{2,1,0:T(8,128)(2,1)S(1)}, bf16[4,8192,128]{2,1,0:T(8,128)(2,1)S(1)}, bf16[4,8192,128]{2,1,0:T(8,128)(2,1)S(1)}) custom-call(s32[4]{0:T(128)} %pos.1, bf16[4,8192]{1,0:T(4,128)(2,1)} %x.1, bf16[8192,8192]{1,0:T(8,128)(2,1)} %wq.1, bf16[8192,1024]{1,0:T(8,128)(2,1)} %wk.1, ...), custom_call_target="tpu_custom_call" | custom-call | tf_op jit(solution)/shard_map/decode/pallas_call | solution.py:315
  34.5 0.0 copy-done
  34.5 6.5 %store.1 = (bf16[4,8192,128]{2,1,0:T(8,128)(2,1)}, bf16[4,8192,128]{2,1,0:T(8,128)(2,1)}, bf16[32,8,128]{2,1,0:T(8,128)(2,1)}, bf16[4,8192,128]{2,1,0:T(8,128)(2,1)S(1)}, bf16[4,8192,128]{2,1,0:T(8,128)(2,1)S(1)}) custom-call(s32[4]{0:T(128)S(1)} %copy-done, ...), custom_call_target="tpu_custom_call", output_to_operand_aliasing={{3}: (3, {}), {4}: (4, {})} | custom-call | tf_op jit(solution)/shard_map/store/pallas_call | solution.py:328
Async XLA Ops:
  0.6 33.9 %copy-start = (s32[4]{0:T(128)S(1)}, s32[4]{0:T(128)}, u32[]{:S(2)}) copy-start(s32[4]{0:T(128)} %pos.1) | copy-start | bytes 52

commit v3 on v2

--- a/solution.py
+++ b/solution.py
@@ -12,21 +12,32 @@
 BF16 = jnp.bfloat16
 NQ = 8
 CT = 1024
+CUT = 1
 CH = 512
 R = 9
 
 
+def torus(n):
+    side = max(1, math.isqrt(n // 2))
+    return n // (2 * side), side
+
+
 def peer(n, k):
-    return lax.rem(lax.axis_index('sp') + k, n)
+    rows, side = torus(n)
+    me = lax.axis_index('sp')
+    core = lax.rem(me + k % 2, 2)
+    col = lax.rem(lax.rem(lax.div(me, 2), side) + k // 2 % side, side)
+    row = lax.rem(lax.div(me, 2 * side) + k // (2 * side), rows)
+    return (row * side + col) * 2 + core
 
 
 def far_first(n, ks):
-    side = max(1, math.isqrt(n // 2))
+    rows, side = torus(n)
 
     def hops(k):
-        a, b = (k // 2) % side, (k // 2) // side
-        return min(a, side - a) + min(b, side - b)
-    return sorted(ks, key=lambda k: (-hops(k), k))
+        a, b = k // 2 % side, k // (2 * side)
+        return min(a, side - a) + min(b, rows - b)
+    return sorted(ks, key=lambda k: (-hops(k), k % 2, k))
 
 
 def barrier(n):
@@ -41,25 +52,27 @@
 
 
 class Softmax:
-    def __init__(self, q2, kt, vb, lim, s_ref, hk):
+    def __init__(self, q2, kt, vb, row0, lim, s_ref, hk):
         nh, dh = q2.shape[0] // 2, q2.shape[1] // 2
-        self.nh, self.dh, self.kt, self.vb, self.lim, self.s = nh, dh, kt, vb, lim, s_ref
+        self.nh, self.dh, self.kt, self.vb, self.lim, self.s = nh, dh, kt, vb, lim - row0, s_ref
+        self.row0 = row0
         self.c2 = dh ** -0.5 * math.log2(math.e)
         self.q2 = q2
         row = lax.broadcasted_iota(jnp.int32, (nh, 128), 0) // hk
         self.lane = lax.broadcasted_iota(jnp.int32, (nh, 128), 1)
-        self.bias = jnp.where(row == lax.rem(self.lane, hk), 0.0, -jnp.inf)
+        self.lane = jnp.where(row == lax.rem(self.lane, hk), self.lane, 2**30)
         self.mx = jnp.full((nh, 128), -jnp.inf, F32)
         self.l = jnp.zeros((nh, 128), F32)
         self.o = jnp.zeros((2 * nh, 2 * dh), F32)
 
     def scores(self, i):
         nh, half = self.nh, CH // 2
-        k2 = jnp.concatenate([self.kt[:, i:i + half], self.kt[:, i + half:i + CH]], axis=0)
+        r = self.row0 + i
+        k2 = jnp.concatenate([self.kt[:, r:r + half], self.kt[:, r + half:r + CH]], axis=0)
         s = jnp.dot(self.q2[...], k2, preferred_element_type=F32)
         for u in range(2):
             for e in range(0, half, 128):
-                se = jnp.where(self.lane < self.lim - (i + u * half + e), s[u * nh:(u + 1) * nh, e:e + 128] + self.bias, -jnp.inf)
+                se = jnp.where(self.lane < self.lim - (i + u * half + e), s[u * nh:(u + 1) * nh, e:e + 128], -jnp.inf)
                 self.mx = jnp.maximum(self.mx, se)
                 self.s[u * nh:(u + 1) * nh, i // 2 + e:i // 2 + e + 128] = se
 
@@ -77,12 +90,20 @@
                 self.l = self.l + p
                 row.append(p.astype(BF16))
             ps.append(jnp.concatenate(row, axis=1))
-        v2 = jnp.concatenate([self.vb[i:i + half], self.vb[i + half:i + CH]], axis=1)
+        r = self.row0 + i
+        v2 = jnp.concatenate([self.vb[r:r + half], self.vb[r + half:r + CH]], axis=1)
         self.o = self.o + jnp.dot(jnp.concatenate(ps, axis=0), v2, preferred_element_type=F32)
 
     def result(self):
         nh, dh = self.nh, self.dh
         return self.m, self.l.sum(1, keepdims=True), self.o[:nh, :dh] + self.o[nh:, dh:]
+
+
+def merge(parts):
+    m = functools.reduce(jnp.maximum, [p[0] for p in parts])
+    safe = jnp.where(m == -jnp.inf, 0.0, m)
+    w = [jnp.exp2(p[0] - safe) for p in parts]
+    return m, sum(a * p[1] for a, p in zip(w, parts)), sum(a * p[2] for a, p in zip(w, parts))
 
 
 def put(n, nb, b, m, l, o, om, ob):
@@ -181,19 +202,22 @@
             q2[b, u * nh:(u + 1) * nh, u * dh:(u + 1) * dh] = qb[b * nh:(b + 1) * nh]
             q2[b, u * nh:(u + 1) * nh, (1 - u) * dh:(2 - u) * dh] = jnp.zeros((nh, dh), BF16)
     g = jnp.zeros((nh, dh), F32)
-    at = [Softmax(q2.at[b], kt.at[b], vv.at[b], (pos[b] - start) * hk, s_ref.at[b % 2], hk) for b in range(nb)]
-    for b in range(nb + 1):
-        if b:
-            ccp[nb + b - 1].wait()
-        for i in range(0, rows, CH):
-            if b < nb:
-                at[b].scores(i)
-            if b:
-                at[b - 1].values(i)
-        if b < nb:
-            at[b].maximum()
-        if b:
-            g = g + put(n, nb, b - 1, *at[b - 1].result(), om, ob)
+    cut = rows // CUT
+    at = [Softmax(q2.at[i // CUT], kt.at[i // CUT], vv.at[i // CUT], i % CUT * cut, (pos[i // CUT] - start) * hk, s_ref.at[i % 2], hk)
+          for i in range(nb * CUT)]
+    for e in range(nb * CUT + 1):
+        if e and (e - 1) % CUT == 0:
+            ccp[nb + (e - 1) // CUT].wait()
+        for i in range(0, cut, CH):
+            if e < nb * CUT:
+                at[e].scores(i)
+            if e:
+                at[e - 1].values(i)
+        if e < nb * CUT:
+            at[e].maximum()
+        if e and e % CUT == 0:
+            b = e // CUT - 1
+            g = g + put(n, nb, b, *merge([a.result() for a in at[b * CUT:e]]), om, ob)
     om[:, 2 * nb, :] = stats_row(n, g, gb)
     cols = wo.shape[1] // n
     for k in far_first(n, range(1, n)):
@@ -230,8 +254,11 @@
     o = jnp.concatenate([o[:nb], o[nb:]], axis=1).astype(BF16)
     wcp_o.wait()
     order = far_first(n, range(n))
-    for g in range(0, n, 8):
-        for k in order[g:g + 8]:
+    cut = sorted({0, n // 8, n // 4, n // 2, 3 * n // 4, n})
+    groups = [order[i:j] for i, j in zip(cut, cut[1:])] + [[]]
+    before = []
+    for group in groups:
+        for k in group:
             to = peer(n, k)
             w = wob[:, pl.ds(pl.multiple_of(to * cols, cols), cols)]
             part = jnp.dot(o, w, preferred_element_type=F32)
@@ -240,10 +267,11 @@
                 ys[to] = part
             else:
                 yrx[me] = part
-        for k in order[g:g + 8]:
+        for k in before:
             if k:
                 to = peer(n, k)
                 pltpu.make_async_remote_copy(ys.at[to], yrx.at[me], ys_, yr_, device_id={'sp': to}, device_id_type=MESH).start()
+        before = group
     all_of(ys.at[pl.ds(0, n - 1)], ys_)
     all_of(yrx.at[pl.ds(0, n - 1)], yr_)
     yb[...] = yrx[...].sum(0).astype(BF16)
@@ -270,8 +298,10 @@
 
         @pl.when(here if own else jnp.logical_not(here))
         def _():
-            for a in bulk(b):
-                a.start()
+            for i in range(0, rows, rows // 16):
+                cut = pl.ds(i, rows // 16)
+                pltpu.make_async_copy(k2.at[b, cut], ko.at[b, cut], sem.at[0, b]).start()
+                pltpu.make_async_copy(v2.at[b, cut], vo.at[b, cut], sem.at[1, b]).start()
     for b in range(nb):
         at = pos[b] - start
 

time: 41.2 us -> 40.6 us (0.985)
  Pallas kernels: 40.4 us -> 39.9 us
    pallas_call x1, Pallas kernels: 33.9 us -> 33.5 us  [local(): pl.pallas_call(functools.partial(decode, n), out_shape=[pltpu.VMEM((n,) +...]
where the time goes in v3:
time: 40.6 us; the launch traced here: 40.5 us
  Pallas kernels  39.9 us (98%)
  between operations  0.66 us (2%)
    pallas_call x1, Pallas kernels, local(): pl.pallas_call(functools.partial(decode, n), out_shape=[pltpu.VMEM((n,) +...  33.5 us
    pallas_call x1, Pallas kernels, local(): pl.pallas_call(functools.partial(store, n), out_shape=[jax.ShapeDtypeStru...  6.42 us

profile of v3, /device:TPU:97, one launch (start us, length us, event | category | flops | bytes accessed | tf_op | source)
XLA Modules:
  0.0 40.5 jit_solution(5954576714189659926)
XLA Ops:
  0.6 0.0 copy-start
  0.6 33.5 %decode.1 = (bf16[32,8,128]{2,1,0:T(8,128)(2,1)S(1)}, bf16[8,8,128]{2,1,0:T(8,128)(2,1)S(1)}, bf16[4,8192,128]{2,1,0:T(8,128)(2,1)S(1)}, bf16[4,8192,128]{2,1,0:T(8,128)(2,1)S(1)}) custom-call(s32[4]{0:T(128)} %pos.1, bf16[4,8192]{1,0:T(4,128)(2,1)} %x.1, bf16[8192,8192]{1,0:T(8,128)(2,1)} %wq.1, bf16[8192,1024]{1,0:T(8,128)(2,1)} %wk.1, ...), custom_call_target="tpu_custom_call" | custom-call | tf_op jit(solution)/shard_map/decode/pallas_call | solution.py:345
  34.1 0.0 copy-done
  34.1 6.4 %store.1 = (bf16[4,8192,128]{2,1,0:T(8,128)(2,1)}, bf16[4,8192,128]{2,1,0:T(8,128)(2,1)}, bf16[32,8,128]{2,1,0:T(8,128)(2,1)}, bf16[4,8192,128]{2,1,0:T(8,128)(2,1)S(1)}, bf16[4,8192,128]{2,1,0:T(8,128)(2,1)S(1)}) custom-call(s32[4]{0:T(128)S(1)} %copy-done, ...), custom_call_target="tpu_custom_call", output_to_operand_aliasing={{3}: (3, {}), {4}: (4, {})} | custom-call | tf_op jit(solution)/shard_map/store/pallas_call | solution.py:358
Async XLA Ops:
  0.6 33.5 %copy-start = (s32[4]{0:T(128)S(1)}, s32[4]{0:T(128)}, u32[]{:S(2)}) copy-start(s32[4]{0:T(128)} %pos.1) | copy-start | bytes 52

commit v4 on v3

--- a/solution.py
+++ b/solution.py
@@ -288,6 +288,7 @@
     hk = rw.shape[1]
     sl = rows // hk
     start = lax.axis_index('sp') * sl
+    pos = [pos[0, b] for b in range(nb)]
 
     def bulk(b):
         return (pltpu.make_async_copy(k2.at[b], ko.at[b], sem.at[0, b]), pltpu.make_async_copy(v2.at[b], vo.at[b], sem.at[1, b]))
@@ -359,10 +360,10 @@
             functools.partial(store, n),
             out_shape=[jax.ShapeDtypeStruct(shape, BF16), jax.ShapeDtypeStruct(shape, BF16), jax.ShapeDtypeStruct(y.shape, BF16),
                        pltpu.VMEM(shape, BF16), pltpu.VMEM(shape, BF16)],
-            in_specs=[sm, vm, vm, vm, vm], out_specs=[hbm, hbm, hbm, vm, vm],
+            in_specs=[vm, vm, vm, vm, vm], out_specs=[hbm, hbm, hbm, vm, vm],
             input_output_aliases={3: 3, 4: 4},
             scratch_shapes=[dma((2, nb)), dma],
-            compiler_params=params(None, 4), name='store')(pos, rw, y, kv, vv)
+            compiler_params=params(None, 4), name='store')(pos.reshape(1, nb), rw, y, kv, vv)
         y = y.reshape(n, 2, nb, dh).transpose(2, 0, 1, 3).reshape(nb, -1)
         return y, ko.reshape(nb, sl, hk, dh), vo.reshape(nb, sl, hk, dh)
 

time: 40.6 us -> 40.2 us (level)
  Pallas kernels: 39.9 us -> 39.4 us
    pallas_call x1, Pallas kernels: 6.42 us -> 5.95 us  [local(): pl.pallas_call(functools.partial(store, n), out_shape=[jax.ShapeDtypeStru...]
where the time goes in v4:
time: 40.2 us; the launch traced here: 40.1 us
  Pallas kernels  39.4 us (98%)
  between operations  0.66 us (2%)
    pallas_call x1, Pallas kernels, local(): pl.pallas_call(functools.partial(decode, n), out_shape=[pltpu.VMEM((n,) +...  33.5 us
    pallas_call x1, Pallas kernels, local(): pl.pallas_call(functools.partial(store, n), out_shape=[jax.ShapeDtypeStru...  5.95 us

profile of v4, /device:TPU:97, one launch (start us, length us, event | category | flops | bytes accessed | tf_op | source)
XLA Modules:
  0.0 40.1 jit_solution(1292380360215836669)
XLA Ops:
  0.6 0.0 copy-start
  0.6 33.5 %decode.1 = (bf16[32,8,128]{2,1,0:T(8,128)(2,1)S(1)}, bf16[8,8,128]{2,1,0:T(8,128)(2,1)S(1)}, bf16[4,8192,128]{2,1,0:T(8,128)(2,1)S(1)}, bf16[4,8192,128]{2,1,0:T(8,128)(2,1)S(1)}) custom-call(s32[4]{0:T(128)} %posh.1, bf16[4,8192]{1,0:T(4,128)(2,1)} %x.1, bf16[8192,8192]{1,0:T(8,128)(2,1)} %wq.1, bf16[8192,1024]{1,0:T(8,128)(2,1)} %wk.1, ...), custom_call_target="tpu_custom_call" | custom-call | tf_op jit(solution)/shard_map/decode/pallas_call | solution.py:346
  34.1 0.0 copy-done
  34.1 6.0 %store.1 = (bf16[4,8192,128]{2,1,0:T(8,128)(2,1)}, bf16[4,8192,128]{2,1,0:T(8,128)(2,1)}, bf16[32,8,128]{2,1,0:T(8,128)(2,1)}, bf16[4,8192,128]{2,1,0:T(8,128)(2,1)S(1)}, bf16[4,8192,128]{2,1,0:T(8,128)(2,1)S(1)}) custom-call(s32[1,4]{1,0:T(1,128)S(1)} %bitcast.10, ...), custom_call_target="tpu_custom_call", output_to_operand_aliasing={{3}: (3, {}), {4}: (4, {})} | custom-call | tf_op jit(solution)/shard_map/store/pallas_call | solution.py:359
Async XLA Ops:
  0.6 33.5 %copy-start = (s32[4]{0:T(128)S(1)}, s32[4]{0:T(128)}, u32[]{:S(2)}) copy-start(s32[4]{0:T(128)} %posh.1) | copy-start | bytes 52
